TPU v7x, 32 devices: a whole 2x2x4 slice. The times are simulated.
32 devices in a mesh: blk: 16 (over z, y, core), tp: 2 (over x).
Axes of the slice: x: 2, y: 2, z: 4, core: 2. Of those that a mesh axis runs over, the one named last changes fastest.
Arguments:
- dec_states: bfloat16 [4096, 5120], P('blk', 'tp'), may hold values from -200 to 200
- norm_gain: float32 [5120], replicated, may hold values from 0.1 to 1.9
- query_weight: bfloat16 [5120, 768], P(None, 'tp'), may hold values from -0.078125 to 0.078125
- out_weight: bfloat16 [768, 5120], P('tp'), may hold values from -0.21875 to 0.21875
- enc_keys: bfloat16 [6144, 768], P('blk', 'tp'), may hold values from -1000 to 1000
- enc_values: bfloat16 [6144, 768], P('blk', 'tp'), may hold values from -6 to 6
Outputs:
- attn_out: bfloat16 [4096, 5120], P('blk', 'tp')
All inputs are finite; a program needn't handle non-finite values.
Results may differ from a plain program's by a relative error of at most 0.034.
Values may be sent and summed in bfloat16 or wider, within the bound.
A program may use at most 128 MiB of HBM per device.

v0:
```python
import math

import jax
import jax.numpy as jnp
from jax import lax
from jax.sharding import PartitionSpec as P

HEAD_DIM = 128


NORM_EPS = 1e-06


def block_rows(total_rows, shard_rows, limit):
    shards = total_rows // shard_rows
    chosen = 1
    for count_try in range(1, shards + 1):
        if shards % count_try == 0 and count_try * shard_rows <= limit:
            chosen = count_try
    return chosen * shard_rows


def per_device(dec_states, norm_gain, query_weight, out_weight, enc_keys, enc_values):
    heads = query_weight.shape[1] // HEAD_DIM
    q_rows = dec_states.shape[0]
    score_scale = 1.0 / math.sqrt(HEAD_DIM)
    states = lax.all_gather(dec_states, "tp", axis=1, tiled=True).astype(jnp.float32)
    mean_sq = jnp.mean(states * states, axis=1, keepdims=True)
    normed = (states * lax.rsqrt(mean_sq + NORM_EPS) * norm_gain).astype(jnp.bfloat16)
    queries = jnp.dot(normed, query_weight, preferred_element_type=jnp.float32).astype(jnp.bfloat16)
    query_heads = queries.reshape(q_rows, heads, HEAD_DIM)
    shard_rows = enc_keys.shape[0]
    start_state = (
        jnp.full((heads, q_rows), -1e30, jnp.float32),
        jnp.zeros((heads, q_rows), jnp.float32),
        jnp.zeros((heads, q_rows, HEAD_DIM), jnp.float32),
    )
    key_rows = lax.all_gather(enc_keys, "blk", axis=0, tiled=True)
    value_rows = lax.all_gather(enc_values, "blk", axis=0, tiled=True)
    count = key_rows.shape[0]
    width_rows = block_rows(count, shard_rows, 1536)
    key_blocks = key_rows.reshape(count // width_rows, width_rows, heads, HEAD_DIM)
    value_blocks = value_rows.reshape(count // width_rows, width_rows, heads, HEAD_DIM)

    def step_block(state, blocks):
        row_max, row_sum, summed = state
        key_block, value_block = blocks
        scores = (
            jnp.einsum("qhd,khd->hqk", query_heads, key_block, preferred_element_type=jnp.float32)
            * score_scale
        )
        new_max = jnp.maximum(row_max, jnp.max(scores, axis=2))
        factor = jnp.exp(row_max - new_max)
        exp_scores = jnp.exp(scores - new_max[:, :, None])
        new_sum = row_sum * factor + jnp.sum(exp_scores, axis=2)
        mixed = jnp.einsum(
            "hqk,khd->hqd",
            exp_scores.astype(jnp.bfloat16),
            value_block,
            preferred_element_type=jnp.float32,
        )
        return ((new_max, new_sum, summed * factor[:, :, None] + mixed), None)

    result, unused = lax.scan(step_block, start_state, (key_blocks, value_blocks))
    row_max, row_sum, summed = result
    attended = (
        (summed / row_sum[:, :, None])
        .transpose(1, 0, 2)
        .reshape(q_rows, heads * HEAD_DIM)
        .astype(jnp.bfloat16)
    )
    partial_out = jnp.dot(attended, out_weight, preferred_element_type=jnp.float32)
    return lax.psum_scatter(partial_out.astype(jnp.bfloat16), "tp", scatter_dimension=1, tiled=True)


def solution(mesh):
    in_specs = (P("blk", "tp"), P(), P(None, "tp"), P("tp", None), P("blk", "tp"), P("blk", "tp"))
    out_specs = P("blk", "tp")
    return jax.shard_map(
        per_device, mesh=mesh, in_specs=in_specs, out_specs=out_specs, check_vma=False
    )
```

profile of v0, /device:TPU:0, one launch (start us, length us, event | category | flops | bytes accessed | tf_op | source)
XLA Modules:
  0.0 269.0 jit_solution(2074089705996655652)
XLA Ops:
  6.5 0.7 all-gather.6.cloned.1.call-update
  7.3 0.7 all-gather.4.cloned.1.call-update
  8.1 0.7 all-gather.8.cloned.1.call-update
  8.8 41.8 %all-gather.6.cloned.1.call-done = bf16[256,5120]{1,0:T(8,128)(2,1)} async-done(((bf16[256,2560]{1,0:T(8,128)(2,1)}), bf16[256,5120]{1,0:T(8,128)(2,1)}) %all-gather.6.cloned.1.call-update) | async-done | bytes 2621456 | tf_op jit(solution)/shard_map/all_gather | solution.py:27
  50.6 2.3 fusion.19
  53.0 4.5 %fusion.26 = bf16[256,384]{1,0:T(8,128)(2,1)S(1)} fusion(bf16[5120,384]{1,0:T(8,128)(2,1)} %param.10, bf16[256,5120]{1,0:T(8,128)(2,1)} %all-gather.6.cloned.1.call-done, f32[5120]{0:T(1024)} %param.9, f32[256]{0:T(256)S(1)} %add_rsqrt_fusion), kind=kOutput, calls=%fused_computation.31 | convolution fusion | flops 1011974144 | bytes 6771712 | tf_op jit(solution)/shard_map/dot_general | solution.py:30
  57.8 48.3 %all-gather.4.cloned.1.call-done = bf16[6144,384]{1,0:T(8,128)(2,1)} async-done(((bf16[384,384]{1,0:T(8,128)(2,1)}), bf16[6144,384]{1,0:T(8,128)(2,1)}) %all-gather.4.cloned.1.call-update) | async-done | bytes 4718608 | tf_op jit(solution)/shard_map/all_gather | solution.py:38
  106.1 13.0 %reshape.26 = bf16[4,1536,3,128]{3,2,1,0:T(4,128)(2,1)} reshape(bf16[6144,384]{1,0:T(8,128)(2,1)} %all-gather.4.cloned.1.call-done) | data formatting | bytes 9437184 | tf_op jit(solution)/shard_map/reshape | solution.py:42
  119.0 6.0 %copy.13 = bf16[4,1536,3,128]{3,1,2,0:T(8,128)(2,1)} copy(bf16[4,1536,3,128]{3,2,1,0:T(4,128)(2,1)} %reshape.26) | data formatting | bytes 9437184
  125.0 35.0 %all-gather.8.cloned.1.call-done = bf16[6144,384]{1,0:T(8,128)(2,1)} async-done(((bf16[384,384]{1,0:T(8,128)(2,1)}), bf16[6144,384]{1,0:T(8,128)(2,1)}) %all-gather.8.cloned.1.call-update) | async-done | bytes 4718608 | tf_op jit(solution)/shard_map/all_gather | solution.py:39
  160.1 12.9 %reshape.27 = bf16[4,1536,3,128]{3,2,1,0:T(4,128)(2,1)} reshape(bf16[6144,384]{1,0:T(8,128)(2,1)} %all-gather.8.cloned.1.call-done) | data formatting | bytes 9437184 | tf_op jit(solution)/shard_map/reshape | solution.py:43
  173.0 6.0 %copy.15 = bf16[4,1536,3,128]{3,1,2,0:T(8,128)(2,1)} copy(bf16[4,1536,3,128]{3,2,1,0:T(4,128)(2,1)} %reshape.27) | data formatting | bytes 9437184
  179.0 41.7 %while.15 = (s32[]{:T(128)}, f32[3,256]{1,0:T(4,128)S(1)}, f32[3,256]{1,0:T(4,128)S(1)}, f32[3,256,128]{2,1,0:T(8,128)S(1)}, bf16[4,1536,3,128]{3,1,2,0:T(8,128)...) while((s32[]{:T(128)}, f32[3,256]{1,0:T(4,128)S(1)}, ...), condition=%wide.region_4.5_spmd.clone, body=%wide.region_1.4_spmd.clone.sunk | while | flops 613715712 | bytes 36422788 | solution.py:64
  179.0 4.2 %bitcast_reduce_fusion.2 = (f32[3,256]{1,0:T(4,128)S(1)}, f32[3,1536,256]{2,1,0:T(8,128)}) fusion(bf16[256,3,128]{2,0,1:T(8,128)(2,1)S(1)} %get-tuple-element.175, bf16[4,1536,3,128]{3,1,2,0:T(8,128)(2,1)} %get-tuple-element.174, s32[]{:T(128)} %get-tuple-element.161), kind=kOutput, calls=%fused_computation.1.clone.1 | convolution fusion | flops 304348416 | bytes 6098432 | tf_op jit(solution)/shard_map/while/body/eval_jaxpr/qhd,khd->hqk/dot_general | solution.py:49
  183.2 3.3 %fusion.42 = f32[3,256]{1,0:T(4,128)S(1)} fusion(f32[3,1536,256]{2,1,0:T(8,128)} %get-tuple-element.149, f32[3,256]{1,0:T(4,128)S(1)} %select_maximum_fusion.2), kind=kLoop, calls=%fused_computation.4.clone.1 | loop fusion | flops 3538176 | bytes 4724736 | tf_op jit(solution)/shard_map/while/body/eval_jaxpr/reduce_sum | solution.py:55
  186.4 0.5 copy-done
  186.9 2.5 fusion.44
  189.4 4.2 %bitcast_reduce_fusion.2 = (f32[3,256]{1,0:T(4,128)S(1)}, f32[3,1536,256]{2,1,0:T(8,128)}) fusion(bf16[256,3,128]{2,0,1:T(8,128)(2,1)S(1)} %get-tuple-element.175, bf16[4,1536,3,128]{3,1,2,0:T(8,128)(2,1)} %get-tuple-element.174, s32[]{:T(128)} %get-tuple-element.161), kind=kOutput, calls=%fused_computation.1.clone.1 | convolution fusion | flops 304348416 | bytes 6098432 | tf_op jit(solution)/shard_map/while/body/eval_jaxpr/qhd,khd->hqk/dot_general | solution.py:49
  193.6 3.3 %fusion.42 = f32[3,256]{1,0:T(4,128)S(1)} fusion(f32[3,1536,256]{2,1,0:T(8,128)} %get-tuple-element.149, f32[3,256]{1,0:T(4,128)S(1)} %select_maximum_fusion.2), kind=kLoop, calls=%fused_computation.4.clone.1 | loop fusion | flops 3538176 | bytes 4724736 | tf_op jit(solution)/shard_map/while/body/eval_jaxpr/reduce_sum | solution.py:55
  196.9 0.5 copy-done
  197.3 2.5 fusion.44
  199.9 4.2 %bitcast_reduce_fusion.2 = (f32[3,256]{1,0:T(4,128)S(1)}, f32[3,1536,256]{2,1,0:T(8,128)}) fusion(bf16[256,3,128]{2,0,1:T(8,128)(2,1)S(1)} %get-tuple-element.175, bf16[4,1536,3,128]{3,1,2,0:T(8,128)(2,1)} %get-tuple-element.174, s32[]{:T(128)} %get-tuple-element.161), kind=kOutput, calls=%fused_computation.1.clone.1 | convolution fusion | flops 304348416 | bytes 6098432 | tf_op jit(solution)/shard_map/while/body/eval_jaxpr/qhd,khd->hqk/dot_general | solution.py:49
  204.0 3.3 %fusion.42 = f32[3,256]{1,0:T(4,128)S(1)} fusion(f32[3,1536,256]{2,1,0:T(8,128)} %get-tuple-element.149, f32[3,256]{1,0:T(4,128)S(1)} %select_maximum_fusion.2), kind=kLoop, calls=%fused_computation.4.clone.1 | loop fusion | flops 3538176 | bytes 4724736 | tf_op jit(solution)/shard_map/while/body/eval_jaxpr/reduce_sum | solution.py:55
  207.3 0.5 copy-done
  207.8 2.5 fusion.44
  210.3 4.2 %bitcast_reduce_fusion.2 = (f32[3,256]{1,0:T(4,128)S(1)}, f32[3,1536,256]{2,1,0:T(8,128)}) fusion(bf16[256,3,128]{2,0,1:T(8,128)(2,1)S(1)} %get-tuple-element.175, bf16[4,1536,3,128]{3,1,2,0:T(8,128)(2,1)} %get-tuple-element.174, s32[]{:T(128)} %get-tuple-element.161), kind=kOutput, calls=%fused_computation.1.clone.1 | convolution fusion | flops 304348416 | bytes 6098432 | tf_op jit(solution)/shard_map/while/body/eval_jaxpr/qhd,khd->hqk/dot_general | solution.py:49
  214.5 3.3 %fusion.42 = f32[3,256]{1,0:T(4,128)S(1)} fusion(f32[3,1536,256]{2,1,0:T(8,128)} %get-tuple-element.149, f32[3,256]{1,0:T(4,128)S(1)} %select_maximum_fusion.2), kind=kLoop, calls=%fused_computation.4.clone.1 | loop fusion | flops 3538176 | bytes 4724736 | tf_op jit(solution)/shard_map/while/body/eval_jaxpr/reduce_sum | solution.py:55
  217.8 0.5 copy-done
  218.2 2.5 fusion.44
  220.7 0.2 copy.16
  220.9 5.2 %convolution_convert_fusion = bf16[256,5120]{1,0:T(8,128)(2,1)} fusion(bf16[256,384]{0,1:T(8,128)(2,1)S(1)} %bitcast.40, bf16[384,5120]{1,0:T(8,128)(2,1)} %param.11), kind=kOutput, calls=%fused_computation.24 | convolution fusion | flops 1007943680 | bytes 6750208 | tf_op jit(solution)/shard_map/dot_general | solution.py:72
  226.1 36.4 %reduce-scatter.2.cloned.1.call-done = bf16[256,2560]{1,0:T(8,128)(2,1)} async-done(((bf16[256,5120]{1,0:T(8,128)(2,1)}), bf16[256,2560]{1,0:T(8,128)(2,1)}) %reduce-scatter.2.cloned.1.call-update) | async-done | bytes 1310736 | tf_op jit(solution)/shard_map/reduce_scatter | solution.py:73
  (28 shorter events, 0.6 us)
Async XLA Ops:
  6.5 44.1 %all-gather.6.cloned.1.call-start = ((), (), s32[]{:S(2)}) async-start(), calls=%async_computation.2 | async-start | bytes 3932160 | tf_op jit(solution)/shard_map/all_gather | solution.py:27
  7.3 98.8 %all-gather.4.cloned.1.call-start = ((), (), s32[]{:S(2)}) async-start(), calls=%async_computation.1 | async-start | bytes 5013504 | tf_op jit(solution)/shard_map/all_gather | solution.py:38
  8.0 152.0 %all-gather.8.cloned.1.call-start = ((), (), s32[]{:S(2)}) async-start(), calls=%async_computation.3 | async-start | bytes 5013504 | tf_op jit(solution)/shard_map/all_gather | solution.py:39
  8.7 253.8 %reduce-scatter.2.cloned.1.call-start = ((), (), s32[]{:S(2)}) async-start(), calls=%async_computation.4 | async-start | bytes 3932160 | tf_op jit(solution)/shard_map/reduce_scatter | solution.py:73
  183.1 3.8 %copy-start = (f32[3,1536,256]{2,1,0:T(8,128)S(1)}, f32[3,1536,256]{2,1,0:T(8,128)}, u32[]{:S(2)}) copy-start(f32[3,1536,256]{2,1,0:T(8,128)} %get-tuple-element.149) | copy-start | bytes 14155780 | tf_op jit(solution)/shard_map/while
  193.6 3.8 %copy-start = (f32[3,1536,256]{2,1,0:T(8,128)S(1)}, f32[3,1536,256]{2,1,0:T(8,128)}, u32[]{:S(2)}) copy-start(f32[3,1536,256]{2,1,0:T(8,128)} %get-tuple-element.149) | copy-start | bytes 14155780 | tf_op jit(solution)/shard_map/while
  204.0 3.8 %copy-start = (f32[3,1536,256]{2,1,0:T(8,128)S(1)}, f32[3,1536,256]{2,1,0:T(8,128)}, u32[]{:S(2)}) copy-start(f32[3,1536,256]{2,1,0:T(8,128)} %get-tuple-element.149) | copy-start | bytes 14155780 | tf_op jit(solution)/shard_map/while
  214.5 3.8 %copy-start = (f32[3,1536,256]{2,1,0:T(8,128)S(1)}, f32[3,1536,256]{2,1,0:T(8,128)}, u32[]{:S(2)}) copy-start(f32[3,1536,256]{2,1,0:T(8,128)} %get-tuple-element.149) | copy-start | bytes 14155780 | tf_op jit(solution)/shard_map/while
Sparse Core Ops, SparseCore 0:
  8.9 41.7 all-gather.5
  52.9 53.1 all-gather.3
  108.4 51.6 all-gather.7
  226.2 36.2 reduce-scatter.1
where the time goes:
time: 270 us; the launch traced here: 269 us
  waiting for transfers between devices  164 us (61%)
  local copies, waits for them, and re-layouts  40.2 us (15%)
  matrix products  36.3 us (13%)
  other arithmetic  15.6 us (6%)
  between operations  13.2 us (5%)
    all_gather x1, waiting for transfers between devices, per_device(): key_rows = lax.all_gather(enc_keys, 'blk', axis=0, tiled=True)  48.3 us
    all_gather x1, waiting for transfers between devices, per_device(): lax.all_gather(dec_states, 'tp', axis=1, tiled=True).astype(jnp.float32)  41.8 us
    reduce_scatter x1, waiting for transfers between devices, per_device(): lax.psum_scatter(partial_out.astype(jnp.bfloat16), 'tp', scatter_dimensio...  36.4 us
    all_gather x1, waiting for transfers between devices, per_device(): value_rows = lax.all_gather(enc_values, 'blk', axis=0, tiled=True)  35 us
    dot_general x4, matrix products, step_block(): jnp.einsum('qhd,khd->hqk', query_heads, key_block, preferred_element_type...  16.7 us
    reduce_sum x4, other arithmetic, step_block(): new_sum = row_sum * factor + jnp.sum(exp_scores, axis=2)  13.1 us
    reshape x1, local copies, waits for them, and re-layouts, per_device(): key_rows.reshape(count // width_rows, width_rows, heads, HEAD_DIM)  13 us
    reshape x1, local copies, waits for them, and re-layouts, per_device(): value_rows.reshape(count // width_rows, width_rows, heads, HEAD_DIM)  12.9 us
  transfers between devices with their start and end apart: 4, of which 4 were waited for; matrix products, arithmetic and copies ran while one was open for 10% of the time, Pallas kernels for 0%

commit v1 on v0

v1 whole, which is shorter than its diff:
```python
import functools
import math

import jax
import jax.numpy as jnp
from jax import lax
from jax.experimental import pallas as pl
from jax.experimental.pallas import tpu as pltpu
from jax.sharding import PartitionSpec as P

HEAD_DIM = 128
NORM_EPS = 1e-06
LANES = 128


def column_tile(width, limit=640):
    best = LANES
    for tile in range(LANES, limit + 1, LANES):
        if width % tile == 0:
            best = tile
    return best


def kernel(
    n_blk,
    n_tp,
    x_hbm,
    gain_ref,
    wq_hbm,
    wo_hbm,
    k_hbm,
    v_hbm,
    out_hbm,
    kbuf,
    vbuf,
    wq,
    wo,
    xbuf,
    xg,
    qsend,
    qrecv,
    own_part,
    sqbuf,
    qbuf,
    attbuf,
    obuf,
    row_max,
    row_sum,
    acc,
    kv_send,
    kv_recv,
    tp_send,
    tp_recv,
    sib_send,
    sib_recv,
    local_sem,
    out_sem,
):
    n_line = n_blk // 4
    b = lax.axis_index("blk")
    t = lax.axis_index("tp")
    core = lax.rem(b, 2)
    side = lax.rem(lax.div(b, 2), 2)
    line = lax.div(b, 4)
    rows = x_hbm.shape[0]
    feat = x_hbm.shape[1]
    width = wq_hbm.shape[1]
    heads = width // HEAD_DIM
    half_feat = feat // 2
    half_width = width // 2

    def index(zz, yy, cc):
        return (zz * 2 + yy) * 2 + cc

    sibling = index(line, side, 1 - core)
    beside = index(line, 1 - side, core)
    peers = [lax.rem(t + off, n_tp) for off in range(1, n_tp)]
    bufs = (kbuf, vbuf)

    def ds(start, size, mult=LANES):
        return pl.ds(pl.multiple_of(start, mult), size)

    loads = [
        pltpu.make_async_copy(k_hbm, kbuf.at[b], local_sem.at[0]),
        pltpu.make_async_copy(v_hbm, vbuf.at[b], local_sem.at[1]),
        pltpu.make_async_copy(x_hbm, xbuf, local_sem.at[2]),
        pltpu.make_async_copy(wq_hbm.at[ds(t * feat, feat)], wq.at[t], local_sem.at[3]),
        pltpu.make_async_copy(wo_hbm.at[:, ds(t * feat, feat)], wo.at[t], local_sem.at[4]),
    ]
    for load in loads:
        load.start()

    barrier = pltpu.get_barrier_semaphore()
    has_left = line > 0
    has_right = line < n_line - 1

    @pl.when(has_left)
    def _():
        pl.semaphore_signal(barrier, inc=1, device_id={"blk": b - 4})

    @pl.when(has_right)
    def _():
        pl.semaphore_signal(barrier, inc=1, device_id={"blk": b + 4})

    pl.semaphore_signal(barrier, inc=1, device_id={"blk": sibling})
    pl.semaphore_signal(barrier, inc=1, device_id={"blk": beside})
    for p in peers:
        pl.semaphore_signal(barrier, inc=1, device_id={"tp": p})

    ends = jnp.where(has_left, 1, 0) + jnp.where(has_right, 1, 0)
    pl.semaphore_wait(barrier, 2 + len(peers) + ends)

    def kv_copy(kv, route, zz, yy, cc, target):
        slot = index(zz, yy, cc)
        return pltpu.make_async_remote_copy(
            src_ref=bufs[kv].at[slot],
            dst_ref=bufs[kv].at[slot],
            send_sem=kv_send.at[kv, route, zz],
            recv_sem=kv_recv.at[kv, slot],
            device_id={"blk": target},
        )

    def right_copy(kv, zz):
        return kv_copy(kv, 0, zz, side, core, b + 4)

    def left_copy(kv, zz):
        return kv_copy(kv, 1, zz, side, core, b - 4)

    def beside_copy(kv, zz):
        return kv_copy(kv, 2, zz, side, core, beside)

    def sib_copy(kv, zz):
        return kv_copy(kv, 3, zz, side, core, sibling)

    def sib_beside_copy(kv, zz):
        return kv_copy(kv, 4, zz, 1 - side, core, sibling)

    def wait_slot(kv, zz, yy, cc):
        kv_copy(kv, 0, zz, yy, cc, sibling).wait_recv()

    def column_event(kv, d):
        if d >= n_line:
            return

        @pl.when(line + d < n_line)
        def _():
            zz = line + d
            wait_slot(kv, zz, side, core)

            @pl.when(has_left)
            def _():
                left_copy(kv, zz).start()

            beside_copy(kv, zz).start()
            sib_copy(kv, zz).start()

        @pl.when(line - d >= 0)
        def _():
            zz = line - d
            wait_slot(kv, zz, side, core)

            @pl.when(has_right)
            def _():
                right_copy(kv, zz).start()

            beside_copy(kv, zz).start()
            sib_copy(kv, zz).start()

    def nearest(k):
        short = jnp.minimum(line, n_line - 1 - line)
        swing = line + (k + 1) // 2 if k % 2 == 1 else line - k // 2
        tail = jnp.where(line < n_line - 1 - line, k, n_line - 1 - k)
        return jnp.where(k <= 2 * short, swing, tail)

    def beside_event(k):
        zz = nearest(k)
        for kv in (0, 1):
            wait_slot(kv, zz, 1 - side, core)
            sib_beside_copy(kv, zz).start()

    def wq_copy(i, p):
        return pltpu.make_async_remote_copy(
            src_ref=wq_hbm.at[ds(p * feat + core * half_feat, half_feat)],
            dst_ref=wq.at[t, ds(core * half_feat, half_feat)],
            send_sem=tp_send.at[0, i],
            recv_sem=tp_recv.at[0, t],
            device_id={"tp": p},
        )

    def wq_landed(p):
        return pltpu.make_async_remote_copy(
            src_ref=wq.at[p, ds(core * half_feat, half_feat)],
            dst_ref=wq.at[p, ds(core * half_feat, half_feat)],
            send_sem=tp_send.at[0, 0],
            recv_sem=tp_recv.at[0, p],
            device_id={"tp": p},
        )

    def wq_sib(p, cc):
        return pltpu.make_async_remote_copy(
            src_ref=wq.at[p, ds(cc * half_feat, half_feat)],
            dst_ref=wq.at[p, ds(cc * half_feat, half_feat)],
            send_sem=sib_send.at[0, p],
            recv_sem=sib_recv.at[0, p],
            device_id={"blk": sibling},
        )

    def wo_copy(i, p):
        return pltpu.make_async_remote_copy(
            src_ref=wo_hbm.at[ds(core * half_width, half_width, 64), ds(p * feat, feat)],
            dst_ref=wo.at[t, ds(core * half_width, half_width, 64)],
            send_sem=tp_send.at[1, i],
            recv_sem=tp_recv.at[1, t],
            device_id={"tp": p},
        )

    def wo_landed(p):
        return pltpu.make_async_remote_copy(
            src_ref=wo.at[p, ds(core * half_width, half_width, 64)],
            dst_ref=wo.at[p, ds(core * half_width, half_width, 64)],
            send_sem=tp_send.at[1, 0],
            recv_sem=tp_recv.at[1, p],
            device_id={"tp": p},
        )

    def wo_sib(p, cc):
        return pltpu.make_async_remote_copy(
            src_ref=wo.at[p, ds(cc * half_width, half_width, 64)],
            dst_ref=wo.at[p, ds(cc * half_width, half_width, 64)],
            send_sem=sib_send.at[1, p],
            recv_sem=sib_recv.at[1, p],
            device_id={"blk": sibling},
        )

    def sq_copy(i, p, slot):
        return pltpu.make_async_remote_copy(
            src_ref=sqbuf.at[slot],
            dst_ref=sqbuf.at[slot],
            send_sem=tp_send.at[2, i],
            recv_sem=tp_recv.at[2, slot],
            device_id={"tp": p},
        )

    def q_copy(i, p, slot):
        return pltpu.make_async_remote_copy(
            src_ref=qsend.at[p],
            dst_ref=qrecv.at[slot],
            send_sem=tp_send.at[3, i],
            recv_sem=tp_recv.at[3, slot],
            device_id={"tp": p},
        )

    def att_copy(i, p, slot):
        return pltpu.make_async_remote_copy(
            src_ref=attbuf.at[slot],
            dst_ref=attbuf.at[slot],
            send_sem=tp_send.at[4, i],
            recv_sem=tp_recv.at[4, slot],
            device_id={"tp": p},
        )

    for i, p in enumerate(peers):
        wq_copy(i, p).start()
    for kv in (0, 1):
        loads[kv].wait()

        @pl.when(has_left)
        def _():
            left_copy(kv, line).start()

        @pl.when(has_right)
        def _():
            right_copy(kv, line).start()

        beside_copy(kv, line).start()
        sib_copy(kv, line).start()

    loads[2].wait()
    tile = column_tile(feat)
    squares = jnp.zeros((rows, 1), jnp.float32)
    for start in range(0, feat, tile):
        piece = xbuf[:, start : start + tile].astype(jnp.float32)
        squares += jnp.sum(piece * piece, axis=1, keepdims=True)
        gain = gain_ref[:, ds(t * feat + start, tile)]
        xg[:, start : start + tile] = (piece * gain).astype(jnp.bfloat16)
    wide = jnp.broadcast_to(squares, (rows, LANES))
    sqbuf[t] = jnp.transpose(wide)[0:8, :]
    loads[3].wait()
    own_part[...] = jnp.dot(xg[...], wq[t], preferred_element_type=jnp.float32)
    for i, p in enumerate(peers):
        sq_copy(i, p, t).start()
    row_max[...] = jnp.full(row_max.shape, -1e30, jnp.float32)
    row_sum[...] = jnp.zeros(row_sum.shape, jnp.float32)
    acc[...] = jnp.zeros(acc.shape, jnp.float32)

    column_event(0, 1)
    column_event(1, 1)
    beside_event(0)
    column_event(0, 2)

    for p in peers:
        wq_landed(p).wait_recv()
        wq_sib(p, core).start()
    for i, p in enumerate(peers):
        wq_sib(p, 1 - core).wait_recv()
        qsend[p] = jnp.dot(xg[...], wq[p], preferred_element_type=jnp.float32).astype(
            jnp.bfloat16
        )
        q_copy(i, p, t).start()
    for i, p in enumerate(peers):
        wo_copy(i, p).start()

    column_event(1, 2)

    total = sqbuf[t][0:1, :]
    for i, p in enumerate(peers):
        sq_copy(i, p, p).wait_recv()
        total = total + sqbuf[p][0:1, :]
    column = jnp.transpose(jnp.broadcast_to(total, (LANES, rows)))
    scale = math.log2(math.e) / math.sqrt(HEAD_DIM)
    factor = lax.rsqrt(column / (feat * n_tp) + NORM_EPS) * scale
    for i, p in enumerate(peers):
        q_copy(i, p, p).wait_recv()
    for h in range(heads):
        cols = slice(h * HEAD_DIM, (h + 1) * HEAD_DIM)
        summed = own_part[:, cols]
        for p in peers:
            summed = summed + qrecv[p, :, cols].astype(jnp.float32)
        qbuf[:, cols] = (summed * factor).astype(jnp.bfloat16)

    def attend(zz, yy):
        for kv in (0, 1):
            wait_slot(kv, zz, yy, 1 - core)
        first = index(zz, yy, 0)

        def one_head(h, carry):
            cols = ds(h * HEAD_DIM, HEAD_DIM)
            keys = kbuf[pl.ds(first, 2), :, cols].reshape(-1, HEAD_DIM)
            vals = vbuf[pl.ds(first, 2), :, cols].reshape(-1, HEAD_DIM)
            scores = lax.dot_general(
                qbuf[:, cols], keys, (((1,), (1,)), ((), ())), preferred_element_type=jnp.float32
            )
            old = row_max[h]
            new = jnp.maximum(old, jnp.max(scores, axis=1, keepdims=True))
            weights = jnp.exp2(scores - new[:, 0:1])
            keep = jnp.exp2(old - new)
            row_max[h] = new
            row_sum[h] = row_sum[h] * keep + jnp.sum(weights, axis=1, keepdims=True)
            mixed = jnp.dot(weights.astype(jnp.bfloat16), vals, preferred_element_type=jnp.float32)
            acc[:, cols] = acc[:, cols] * keep + mixed
            return carry

        lax.fori_loop(0, heads, one_head, 0)

    attend(line, side)
    beside_event(1)
    attend(line, 1 - side)
    attend(nearest(1), side)
    for d in range(2, n_line):
        column_event(0, d + 1)
        attend(nearest(d - 1), 1 - side)
        attend(nearest(d), side)
        column_event(1, d + 1)
        beside_event(d)
    for p in peers:
        wo_landed(p).wait_recv()
        wo_sib(p, core).start()
    attend(nearest(n_line - 1), 1 - side)

    for h in range(heads):
        cols = slice(h * HEAD_DIM, (h + 1) * HEAD_DIM)
        attbuf[t, :, cols] = (acc[:, cols] / row_sum[h]).astype(jnp.bfloat16)
    loads[4].wait()
    for p in peers:
        wo_sib(p, 1 - core).wait_recv()
    for i, p in enumerate(peers):
        att_copy(i, p, t).start()
    for i, p in enumerate(peers):
        att_copy(i, p, p).wait_recv()
    stores = []
    for j, start in enumerate(range(0, feat, tile)):
        cols = slice(start, start + tile)
        result = jnp.zeros((rows, tile), jnp.float32)
        for p in range(n_tp):
            result += jnp.dot(attbuf[p], wo[p, :, cols], preferred_element_type=jnp.float32)
        obuf[:, cols] = result.astype(jnp.bfloat16)
        store = pltpu.make_async_copy(obuf.at[:, cols], out_hbm.at[:, cols], out_sem.at[j])
        store.start()
        stores.append(store)

    for kv in (0, 1):
        for zz in range(n_line):

            @pl.when(has_right & (line >= zz))
            def _():
                right_copy(kv, zz).wait_send()

            @pl.when(has_left & (line <= zz))
            def _():
                left_copy(kv, zz).wait_send()

            beside_copy(kv, zz).wait_send()
            sib_copy(kv, zz).wait_send()
            sib_beside_copy(kv, zz).wait_send()
    for i, p in enumerate(peers):
        wq_copy(i, p).wait_send()
        wo_copy(i, p).wait_send()
        sq_copy(i, p, t).wait_send()
        q_copy(i, p, t).wait_send()
        att_copy(i, p, t).wait_send()
        wq_sib(p, core).wait_send()
        wo_sib(p, core).wait_send()
    for store in stores:
        store.wait()


def per_device(n_blk, n_tp, dec_states, norm_gain, query_weight, out_weight, enc_keys, enc_values):
    rows, feat = dec_states.shape
    width = query_weight.shape[1]
    enc_rows = enc_keys.shape[0]
    heads = width // HEAD_DIM
    n_line = n_blk // 4
    tiles = feat // column_tile(feat)
    bf16, f32 = jnp.bfloat16, jnp.float32
    anywhere = pl.BlockSpec(memory_space=pl.ANY)
    return pl.pallas_call(
        functools.partial(kernel, n_blk, n_tp),
        out_shape=jax.ShapeDtypeStruct((rows, feat), bf16),
        in_specs=[
            anywhere,
            pl.BlockSpec(memory_space=pltpu.VMEM),
            anywhere,
            anywhere,
            anywhere,
            anywhere,
        ],
        out_specs=anywhere,
        scratch_shapes=[
            pltpu.VMEM((n_blk, enc_rows, width), bf16),
            pltpu.VMEM((n_blk, enc_rows, width), bf16),
            pltpu.VMEM((n_tp, feat, width), bf16),
            pltpu.VMEM((n_tp, width, feat), bf16),
            pltpu.VMEM((rows, feat), bf16),
            pltpu.VMEM((rows, feat), bf16),
            pltpu.VMEM((n_tp, rows, width), bf16),
            pltpu.VMEM((n_tp, rows, width), bf16),
            pltpu.VMEM((rows, width), f32),
            pltpu.VMEM((n_tp, 8, rows), f32),
            pltpu.VMEM((rows, width), bf16),
            pltpu.VMEM((n_tp, rows, width), bf16),
            pltpu.VMEM((rows, feat), bf16),
            pltpu.VMEM((heads, rows, LANES), f32),
            pltpu.VMEM((heads, rows, LANES), f32),
            pltpu.VMEM((rows, width), f32),
            pltpu.SemaphoreType.DMA((2, 5, n_line)),
            pltpu.SemaphoreType.DMA((2, n_blk)),
            pltpu.SemaphoreType.DMA((5, n_tp)),
            pltpu.SemaphoreType.DMA((5, n_tp)),
            pltpu.SemaphoreType.DMA((2, n_tp)),
            pltpu.SemaphoreType.DMA((2, n_tp)),
            pltpu.SemaphoreType.DMA((5,)),
            pltpu.SemaphoreType.DMA((tiles,)),
        ],
        compiler_params=pltpu.CompilerParams(
            collective_id=0, has_side_effects=True, vmem_limit_bytes=60 * 1024 * 1024
        ),
    )(dec_states, norm_gain.reshape(1, -1), query_weight, out_weight, enc_keys, enc_values)


def solution(mesh):
    in_specs = (P("blk", "tp"), P(), P(None, "tp"), P("tp", None), P("blk", "tp"), P("blk", "tp"))
    out_specs = P("blk", "tp")
    body = functools.partial(per_device, mesh.shape["blk"], mesh.shape["tp"])
    return jax.shard_map(body, mesh=mesh, in_specs=in_specs, out_specs=out_specs, check_vma=False)
```

time: 270 us -> 71.9 us (0.27)
  waiting for transfers between devices: 164 us -> 0 us
  Pallas kernels: 0 us -> 69.2 us
  local copies, waits for them, and re-layouts: 40.2 us -> 2.46 us
  matrix products: 36.3 us -> 0 us
  other arithmetic: 15.6 us -> 0 us
  between operations: 13.2 us -> 0.01 us
    all_gather x3 -> x0, waiting for transfers between devices: 125 us -> none  [the longest x1 48.3 us: per_device(): key_rows = lax.all_gather(enc_keys, 'blk', axis=0, tiled=True)]
    pallas_call x0 -> x1, Pallas kernels: none -> 69.2 us  [per_device(): pl.pallas_call(functools.partial(kernel, n_blk, n_tp), out_shape=jax.Shap...]
    reduce_scatter x1 -> x0, waiting for transfers between devices: 36.4 us -> none  [per_device(): lax.psum_scatter(partial_out.astype(jnp.bfloat16), 'tp', scatter_dimensio...]
    dot_general x10 -> x0, matrix products: 36.3 us -> none  [the longest x4 16.7 us: step_block(): jnp.einsum('qhd,khd->hqk', query_heads, key_block, preferred_element_type...]
    reshape x2 -> x0, local copies, waits for them, and re-layouts: 25.9 us -> none  [the longest x1 13 us: per_device(): key_rows.reshape(count // width_rows, width_rows, heads, HEAD_DIM)]
    reduce_sum x5 -> x0, other arithmetic: 15.4 us -> none  [the longest x4 13.1 us: step_block(): new_sum = row_sum * factor + jnp.sum(exp_scores, axis=2)]
    unnamed x3 -> x1, local copies, waits for them, and re-layouts: 12.2 us -> 2.46 us
  transfers between devices with their start and end apart: 4 -> 0, of which waited for: 4 -> 0; matrix products, arithmetic and copies ran while one was open for 10% -> 0% of each run, Pallas kernels for 0% -> 0%
where the time goes in v1:
time: 71.9 us; the launch traced here: 71.7 us
  Pallas kernels  69.2 us (96%)
  local copies, waits for them, and re-layouts  2.46 us (3%)
    pallas_call x1, Pallas kernels, per_device(): pl.pallas_call(functools.partial(kernel, n_blk, n_tp), out_shape=jax.Shap...  69.2 us
    unnamed x1, local copies, waits for them, and re-layouts  2.46 us

profile of v1, /device:TPU:0, one launch (start us, length us, event | category | flops | bytes accessed | tf_op | source)
XLA Modules:
  0.0 71.7 jit_solution(74629536313054098)
XLA Ops:
  0.0 69.2 %shard_map.64 = bf16[256,2560]{1,0:T(8,128)(2,1)} custom-call(bf16[256,2560]{1,0:T(8,128)(2,1)} %x_hbm.1, f32[1,5120]{1,0:T(1,128)} %bitcast.1, bf16[5120,384]{1,0:T(8,128)(2,1)} %wq_hbm.1, bf16[384,5120]{1,0:T(8,128)(2,1)} %wo_hbm.1, bf16[384,384]{1,0:T(8,128)(2,1)} %k_hbm.1, bf16[384,384]{1,0:T(8,128)(2,1)} %v_hbm.1), custom_call_target="tpu_custom_call" | custom-call | tf_op jit(solution)/shard_map/pallas_call | solution.py:426
  69.2 2.5 %copy.8 = bf16[256,2560]{1,0:T(8,128)(2,1)} copy(bf16[256,2560]{1,0:T(8,128)(2,1)} %shard_map.64) | data formatting | bytes 2621440

commit v2 on v1

v2 whole, which is shorter than its diff:
```python
import functools
import math

import jax
import jax.numpy as jnp
from jax import lax
from jax.experimental import pallas as pl
from jax.experimental.pallas import tpu as pltpu
from jax.sharding import PartitionSpec as P

HEAD_DIM = 128
NORM_EPS = 1e-06
LANES = 128


def column_tile(width, limit=640):
    best = LANES
    for tile in range(LANES, limit + 1, LANES):
        if width % tile == 0:
            best = tile
    return best


def kernel(
    n_blk,
    n_tp,
    x_hbm,
    gain_ref,
    wq_hbm,
    wo_hbm,
    k_hbm,
    v_hbm,
    out_hbm,
    kvbuf,
    wq,
    wo,
    xbuf,
    xg,
    qsend,
    qrecv,
    own_part,
    sqbuf,
    qbuf,
    attbuf,
    oacc,
    obuf,
    kv_send,
    kv_recv,
    move_send,
    tp_send,
    tp_recv,
    head_send,
    head_recv,
    sib_send,
    sib_recv,
    kv_local,
    wo_local,
    local_sem,
    out_sem,
):
    n_line = n_blk // 4
    b = lax.axis_index("blk")
    t = lax.axis_index("tp")
    core = lax.rem(b, 2)
    side = lax.rem(lax.div(b, 2), 2)
    line = lax.div(b, 4)
    rows = x_hbm.shape[0]
    feat = x_hbm.shape[1]
    width = wq_hbm.shape[1]
    heads = width // HEAD_DIM
    pieces = 2 * heads
    half_feat = feat // 2
    half_head = HEAD_DIM // 2
    moved = tuple(range(1, 1 + pieces // 2))
    ahead = 3

    def index(zz, yy, cc):
        return (zz * 2 + yy) * 2 + cc

    sibling = index(line, side, 1 - core)
    beside = index(line, 1 - side, core)
    peers = [lax.rem(t + off, n_tp) for off in range(1, n_tp)]

    def ds(start, size, mult=LANES):
        return pl.ds(pl.multiple_of(start, mult), size)

    def head_cols(h):
        return slice(h * HEAD_DIM, (h + 1) * HEAD_DIM)

    kv_loads = [
        pltpu.make_async_copy(
            (k_hbm, v_hbm)[e % 2].at[:, head_cols(e // 2)], kvbuf.at[e, b], kv_local.at[e]
        )
        for e in range(pieces)
    ]
    wo_loads = [
        pltpu.make_async_copy(
            wo_hbm.at[head_cols(h), ds(t * feat, feat)], wo.at[t, h], wo_local.at[h]
        )
        for h in range(heads)
    ]
    x_load = pltpu.make_async_copy(x_hbm, xbuf, local_sem.at[0])
    wq_load = pltpu.make_async_copy(wq_hbm.at[ds(t * feat, feat)], wq.at[t], local_sem.at[1])
    for load in kv_loads + [x_load, wq_load] + wo_loads:
        load.start()

    barrier = pltpu.get_barrier_semaphore()
    has_left = line > 0
    has_right = line < n_line - 1

    @pl.when(has_left)
    def _():
        pl.semaphore_signal(barrier, inc=1, device_id={"blk": b - 4})

    @pl.when(has_right)
    def _():
        pl.semaphore_signal(barrier, inc=1, device_id={"blk": b + 4})

    pl.semaphore_signal(barrier, inc=1, device_id={"blk": sibling})
    pl.semaphore_signal(barrier, inc=1, device_id={"blk": beside})
    for p in peers:
        pl.semaphore_signal(barrier, inc=1, device_id={"tp": p})
    ends = jnp.where(has_left, 1, 0) + jnp.where(has_right, 1, 0)
    pl.semaphore_wait(barrier, 2 + len(peers) + ends)

    def kv_copy(e, send_sem, slot, target):
        return pltpu.make_async_remote_copy(
            src_ref=kvbuf.at[e, slot],
            dst_ref=kvbuf.at[e, slot],
            send_sem=send_sem,
            recv_sem=kv_recv.at[e, slot],
            device_id={"blk": target},
        )

    def right_copy(e, zz):
        return kv_copy(e, kv_send.at[e, 0, zz], index(zz, side, core), b + 4)

    def left_copy(e, zz):
        return kv_copy(e, kv_send.at[e, 1, zz], index(zz, side, core), b - 4)

    def beside_copy(e, zz):
        return kv_copy(e, kv_send.at[e, 2, zz], index(zz, side, core), beside)

    def sib_copy(e, zz):
        return kv_copy(e, kv_send.at[e, 3, zz], index(zz, side, core), sibling)

    def sib_beside_copy(e, zz):
        return kv_copy(e, kv_send.at[e, 4, zz], index(zz, 1 - side, core), sibling)

    def move_left(e):
        return kv_copy(e, move_send.at[0, e], index(n_line - 1, 1 - side, core), b - 4)

    def move_right(e):
        return kv_copy(e, move_send.at[1, e], index(0, 1 - side, core), b + 4)

    def goes_beside(e, zz):
        inner = (zz > 0) & (zz < n_line - 1)
        return inner | (zz == line) if e in moved else zz >= 0

    def wait_slot(e, slot):
        kv_copy(e, kv_send.at[e, 0, 0], slot, sibling).wait_recv()

    def own_event(e):
        if e >= pieces:
            return
        kv_loads[e].wait()

        @pl.when(has_left)
        def _():
            left_copy(e, line).start()

        @pl.when(has_right)
        def _():
            right_copy(e, line).start()

        beside_copy(e, line).start()
        sib_copy(e, line).start()

    def column_event(e, d):
        @pl.when(line + d < n_line)
        def _():
            zz = line + d
            wait_slot(e, index(zz, side, core))

            @pl.when(has_left)
            def _():
                left_copy(e, zz).start()

            @pl.when(goes_beside(e, zz))
            def _():
                beside_copy(e, zz).start()

            sib_copy(e, zz).start()

        @pl.when(line - d >= 0)
        def _():
            zz = line - d
            wait_slot(e, index(zz, side, core))

            @pl.when(has_right)
            def _():
                right_copy(e, zz).start()

            @pl.when(goes_beside(e, zz))
            def _():
                beside_copy(e, zz).start()

            sib_copy(e, zz).start()

    def move_event(e, d):
        @pl.when(line + d == n_line - 1)
        def _():
            zz = line + d
            wait_slot(e, index(zz, 1 - side, core))

            @pl.when(has_left)
            def _():
                move_left(e).start()

            sib_beside_copy(e, zz).start()

        @pl.when(line - d == 0)
        def _():
            zz = line - d
            wait_slot(e, index(zz, 1 - side, core))

            @pl.when(has_right)
            def _():
                move_right(e).start()

            sib_beside_copy(e, zz).start()

    def nearest(k):
        short = jnp.minimum(line, n_line - 1 - line)
        swing = line + (k + 1) // 2 if k % 2 == 1 else line - k // 2
        tail = jnp.where(line < n_line - 1 - line, k, n_line - 1 - k)
        return jnp.where(k <= 2 * short, swing, tail)

    def beside_event(e, k):
        zz = nearest(k)

        def handle():
            wait_slot(e, index(zz, 1 - side, core))
            sib_beside_copy(e, zz).start()

        if e in moved:
            pl.when((zz > 0) & (zz < n_line - 1))(handle)
        else:
            handle()

    def wave(s):
        for d in range(1, n_line):
            e = s + 1 - d
            if 0 <= e < pieces:
                column_event(e, d)
        own_event(s + ahead)
        for d in range(n_line):
            if s - d in moved:
                move_event(s - d, d)

    n_waves = pieces + n_line - 2

    def tp_copy(src, dst, send_sem, recv_sem, p):
        return pltpu.make_async_remote_copy(
            src_ref=src, dst_ref=dst, send_sem=send_sem, recv_sem=recv_sem, device_id={"tp": p}
        )

    def wq_half(p, cc):
        return wq.at[p, ds(cc * half_feat, half_feat)]

    def wq_copy(i, p):
        src = wq_hbm.at[ds(p * feat + core * half_feat, half_feat)]
        return tp_copy(src, wq_half(t, core), tp_send.at[0, i], tp_recv.at[0, t], p)

    def wq_landed(p):
        ref = wq_half(p, core)
        return tp_copy(ref, ref, tp_send.at[0, 0], tp_recv.at[0, p], p)

    def wq_sib(p, cc):
        return pltpu.make_async_remote_copy(
            src_ref=wq_half(p, cc),
            dst_ref=wq_half(p, cc),
            send_sem=sib_send.at[heads, p],
            recv_sem=sib_recv.at[heads, p],
            device_id={"blk": sibling},
        )

    def wo_half(p, h, cc):
        return wo.at[p, h, ds(cc * half_head, half_head, half_head)]

    def wo_copy(i, p, h):
        src = wo_hbm.at[ds(h * HEAD_DIM + core * half_head, half_head, half_head), ds(p * feat, feat)]
        return tp_copy(src, wo_half(t, h, core), head_send.at[0, h, i], head_recv.at[0, h, t], p)

    def wo_landed(p, h):
        ref = wo_half(p, h, core)
        return tp_copy(ref, ref, head_send.at[0, h, 0], head_recv.at[0, h, p], p)

    def wo_sib(p, h, cc):
        return pltpu.make_async_remote_copy(
            src_ref=wo_half(p, h, cc),
            dst_ref=wo_half(p, h, cc),
            send_sem=sib_send.at[h, p],
            recv_sem=sib_recv.at[h, p],
            device_id={"blk": sibling},
        )

    def sq_copy(i, p, slot):
        ref = sqbuf.at[slot]
        return tp_copy(ref, ref, tp_send.at[1, i], tp_recv.at[1, slot], p)

    def q_copy(i, p, slot):
        return tp_copy(qsend.at[p], qrecv.at[slot], tp_send.at[2, i], tp_recv.at[2, slot], p)

    def att_copy(i, p, h, slot):
        ref = attbuf.at[slot, h]
        return tp_copy(ref, ref, head_send.at[1, h, i], head_recv.at[1, h, slot], p)

    for i, p in enumerate(peers):
        wq_copy(i, p).start()
    for e in range(ahead):
        own_event(e)

    x_load.wait()
    tile = column_tile(feat)
    squares = jnp.zeros((rows, 1), jnp.float32)
    for start in range(0, feat, tile):
        piece = xbuf[:, start : start + tile].astype(jnp.float32)
        squares += jnp.sum(piece * piece, axis=1, keepdims=True)
        gain = gain_ref[:, ds(t * feat + start, tile)]
        xg[:, start : start + tile] = (piece * gain).astype(jnp.bfloat16)
    wide = jnp.broadcast_to(squares, (rows, LANES))
    sqbuf[t] = jnp.transpose(wide)[0:8, :]
    wave(0)
    wq_load.wait()
    own_part[...] = jnp.dot(xg[...], wq[t], preferred_element_type=jnp.float32)
    for i, p in enumerate(peers):
        sq_copy(i, p, t).start()
    weights_wave = n_waves // 2
    for s in range(1, weights_wave):
        wave(s)

    for p in peers:
        wq_landed(p).wait_recv()
        wq_sib(p, core).start()
    for i, p in enumerate(peers):
        wq_sib(p, 1 - core).wait_recv()
        qsend[p] = jnp.dot(xg[...], wq[p], preferred_element_type=jnp.float32).astype(
            jnp.bfloat16
        )
        q_copy(i, p, t).start()
    for h in range(heads - 1):
        for i, p in enumerate(peers):
            wo_copy(i, p, h).start()

    wave(weights_wave)

    total = sqbuf[t][0:1, :]
    for i, p in enumerate(peers):
        sq_copy(i, p, p).wait_recv()
        total = total + sqbuf[p][0:1, :]
    column = jnp.transpose(jnp.broadcast_to(total, (LANES, rows)))
    scale = math.log2(math.e) / math.sqrt(HEAD_DIM)
    factor = lax.rsqrt(column / (feat * n_tp) + NORM_EPS) * scale
    for i, p in enumerate(peers):
        q_copy(i, p, p).wait_recv()
    for h in range(heads):
        summed = own_part[:, head_cols(h)]
        for p in peers:
            summed = summed + qrecv[p, :, head_cols(h)].astype(jnp.float32)
        qbuf[:, head_cols(h)] = (summed * factor).astype(jnp.bfloat16)

    def attend(h, state, zz, yy):
        for e in (2 * h, 2 * h + 1):
            wait_slot(e, index(zz, yy, 1 - core))
        first = index(zz, yy, 0)
        keys = kvbuf[2 * h, pl.ds(first, 2)].reshape(-1, HEAD_DIM)
        vals = kvbuf[2 * h + 1, pl.ds(first, 2)].reshape(-1, HEAD_DIM)
        scores = lax.dot_general(
            qbuf[:, head_cols(h)],
            keys,
            (((1,), (1,)), ((), ())),
            preferred_element_type=jnp.float32,
        )
        old, row_sum, acc = state
        new = jnp.maximum(old, jnp.max(scores, axis=1, keepdims=True))
        weights = jnp.exp2(scores - new)
        keep = jnp.exp2(old - new)
        row_sum = row_sum * keep + jnp.sum(weights, axis=1, keepdims=True)
        mixed = jnp.dot(weights.astype(jnp.bfloat16), vals, preferred_element_type=jnp.float32)
        return new, row_sum, acc * keep + mixed

    def head_attention(h):
        state = (
            jnp.full((rows, 1), -1e30, jnp.float32),
            jnp.zeros((rows, 1), jnp.float32),
            jnp.zeros((rows, HEAD_DIM), jnp.float32),
        )
        for e in (2 * h, 2 * h + 1):
            beside_event(e, 0)
        for k in range(n_line):
            state = attend(h, state, nearest(k), side)
            if k >= 1:
                state = attend(h, state, nearest(k - 1), 1 - side)
            if k + 1 < n_line:
                for e in (2 * h, 2 * h + 1):
                    beside_event(e, k + 1)
        unused, row_sum, acc = attend(h, state, nearest(n_line - 1), 1 - side)
        attbuf[t, h] = (acc / row_sum).astype(jnp.bfloat16)
        for i, p in enumerate(peers):
            att_copy(i, p, h, t).start()

    done = weights_wave + 1
    for h in range(heads):
        need = n_waves if h == heads - 1 else min(2 * h + 1 + n_line, n_waves)
        while done < need:
            wave(done)
            done += 1
        for hh in range(heads - 1):
            if h == heads - 1:
                for p in peers:
                    wo_landed(p, hh).wait_recv()
                    wo_sib(p, hh, core).start()
        head_attention(h)
        if h == 0:
            for i, p in enumerate(peers):
                wo_copy(i, p, heads - 1).start()

    last = heads - 1
    for p in peers:
        wo_landed(p, last).wait_recv()
        wo_sib(p, last, core).start()
    for load in wo_loads:
        load.wait()
    for h in range(heads - 1):
        for i, p in enumerate(peers):
            wo_sib(p, h, 1 - core).wait_recv()
            att_copy(i, p, h, p).wait_recv()
    starts = range(0, feat, tile)
    for start in starts:
        cols = slice(start, start + tile)
        result = jnp.dot(attbuf[t, last], wo[t, last, :, cols], preferred_element_type=jnp.float32)
        for p in range(n_tp):
            for h in range(heads - 1):
                result += jnp.dot(
                    attbuf[p, h], wo[p, h, :, cols], preferred_element_type=jnp.float32
                )
        oacc[:, cols] = result
    for i, p in enumerate(peers):
        wo_sib(p, last, 1 - core).wait_recv()
        att_copy(i, p, last, p).wait_recv()
    stores = []
    for j, start in enumerate(starts):
        cols = slice(start, start + tile)
        result = oacc[:, cols]
        for p in peers:
            result += jnp.dot(
                attbuf[p, last], wo[p, last, :, cols], preferred_element_type=jnp.float32
            )
        obuf[:, cols] = result.astype(jnp.bfloat16)
        store = pltpu.make_async_copy(obuf.at[:, cols], out_hbm.at[:, cols], out_sem.at[j])
        store.start()
        stores.append(store)

    for e in range(pieces):
        for zz in range(n_line):

            @pl.when(has_right & (line >= zz))
            def _():
                right_copy(e, zz).wait_send()

            @pl.when(has_left & (line <= zz))
            def _():
                left_copy(e, zz).wait_send()

            if e in moved and zz in (0, n_line - 1):

                @pl.when(line == zz)
                def _():
                    beside_copy(e, zz).wait_send()

            else:
                beside_copy(e, zz).wait_send()
            sib_copy(e, zz).wait_send()
            sib_beside_copy(e, zz).wait_send()
        if e in moved:

            @pl.when(has_left)
            def _():
                move_left(e).wait_send()

            @pl.when(has_right)
            def _():
                move_right(e).wait_send()

    for i, p in enumerate(peers):
        wq_copy(i, p).wait_send()
        sq_copy(i, p, t).wait_send()
        q_copy(i, p, t).wait_send()
        wq_sib(p, core).wait_send()
        for h in range(heads):
            wo_copy(i, p, h).wait_send()
            att_copy(i, p, h, t).wait_send()
            wo_sib(p, h, core).wait_send()
    for store in stores:
        store.wait()


def per_device(n_blk, n_tp, dec_states, norm_gain, query_weight, out_weight, enc_keys, enc_values):
    rows, feat = dec_states.shape
    width = query_weight.shape[1]
    enc_rows = enc_keys.shape[0]
    heads = width // HEAD_DIM
    n_line = n_blk // 4
    tiles = feat // column_tile(feat)
    bf16, f32 = jnp.bfloat16, jnp.float32
    dma = pltpu.SemaphoreType.DMA
    anywhere = pl.BlockSpec(memory_space=pl.ANY)
    return pl.pallas_call(
        functools.partial(kernel, n_blk, n_tp),
        out_shape=jax.ShapeDtypeStruct((rows, feat), bf16),
        in_specs=[
            anywhere,
            pl.BlockSpec(memory_space=pltpu.VMEM),
            anywhere,
            anywhere,
            anywhere,
            anywhere,
        ],
        out_specs=anywhere,
        scratch_shapes=[
            pltpu.VMEM((2 * heads, n_blk, enc_rows, HEAD_DIM), bf16),
            pltpu.VMEM((n_tp, feat, width), bf16),
            pltpu.VMEM((n_tp, heads, HEAD_DIM, feat), bf16),
            pltpu.VMEM((rows, feat), bf16),
            pltpu.VMEM((rows, feat), bf16),
            pltpu.VMEM((n_tp, rows, width), bf16),
            pltpu.VMEM((n_tp, rows, width), bf16),
            pltpu.VMEM((rows, width), f32),
            pltpu.VMEM((n_tp, 8, rows), f32),
            pltpu.VMEM((rows, width), bf16),
            pltpu.VMEM((n_tp, heads, rows, HEAD_DIM), bf16),
            pltpu.VMEM((rows, feat), f32),
            pltpu.VMEM((rows, feat), bf16),
            dma((2 * heads, 5, n_line)),
            dma((2 * heads, n_blk)),
            dma((2, 2 * heads)),
            dma((3, n_tp)),
            dma((3, n_tp)),
            dma((2, heads, n_tp)),
            dma((2, heads, n_tp)),
            dma((heads + 1, n_tp)),
            dma((heads + 1, n_tp)),
            dma((2 * heads,)),
            dma((heads,)),
            dma((2,)),
            dma((tiles,)),
        ],
        compiler_params=pltpu.CompilerParams(
            collective_id=0, has_side_effects=True, vmem_limit_bytes=60 * 1024 * 1024
        ),
    )(dec_states, norm_gain.reshape(1, -1), query_weight, out_weight, enc_keys, enc_values)


def solution(mesh):
    in_specs = (P("blk", "tp"), P(), P(None, "tp"), P("tp", None), P("blk", "tp"), P("blk", "tp"))
    out_specs = P("blk", "tp")
    body = functools.partial(per_device, mesh.shape["blk"], mesh.shape["tp"])
    return jax.shard_map(body, mesh=mesh, in_specs=in_specs, out_specs=out_specs, check_vma=False)
```

time: 71.9 us -> 73.2 us (1.018)
  Pallas kernels: 69.2 us -> 70.5 us
    pallas_call x1, Pallas kernels: 69.2 us -> 70.5 us  [per_device(): pl.pallas_call(functools.partial(kernel, n_blk, n_tp), out_shape=jax.Shap...]
where the time goes in v2:
time: 73.2 us; the launch traced here: 73 us
  Pallas kernels  70.5 us (96%)
  local copies, waits for them, and re-layouts  2.46 us (3%)
    pallas_call x1, Pallas kernels, per_device(): pl.pallas_call(functools.partial(kernel, n_blk, n_tp), out_shape=jax.Shap...  70.5 us
    unnamed x1, local copies, waits for them, and re-layouts  2.46 us

profile of v2, /device:TPU:0, one launch (start us, length us, event | category | flops | bytes accessed | tf_op | source)
XLA Modules:
  0.0 73.0 jit_solution(3864406344245817153)
XLA Ops:
  0.0 70.5 %shard_map.64 = bf16[256,2560]{1,0:T(8,128)(2,1)} custom-call(bf16[256,2560]{1,0:T(8,128)(2,1)} %x_hbm.1, f32[1,5120]{1,0:T(1,128)} %bitcast.1, bf16[5120,384]{1,0:T(8,128)(2,1)} %wq_hbm.1, bf16[384,5120]{1,0:T(8,128)(2,1)} %wo_hbm.1, bf16[384,384]{1,0:T(8,128)(2,1)} %k_hbm.1, bf16[384,384]{1,0:T(8,128)(2,1)} %v_hbm.1), custom_call_target="tpu_custom_call" | custom-call | tf_op jit(solution)/shard_map/pallas_call | solution.py:519
  70.5 2.5 %copy.8 = bf16[256,2560]{1,0:T(8,128)(2,1)} copy(bf16[256,2560]{1,0:T(8,128)(2,1)} %shard_map.64) | data formatting | bytes 2621440

commit v3 on v2

--- a/solution.py
+++ b/solution.py
@@ -71,7 +71,7 @@
     pieces = 2 * heads
     half_feat = feat // 2
     half_head = HEAD_DIM // 2
-    moved = tuple(range(1, 1 + pieces // 2))
+    moved = ()
     ahead = 3
 
     def index(zz, yy, cc):

time: 73.2 us -> 70.1 us (0.958)
  Pallas kernels: 70.5 us -> 67.4 us
    pallas_call x1, Pallas kernels: 70.5 us -> 67.4 us  [per_device(): pl.pallas_call(functools.partial(kernel, n_blk, n_tp), out_shape=jax.Shap...]
where the time goes in v3:
time: 70.1 us; the launch traced here: 69.9 us
  Pallas kernels  67.4 us (96%)
  local copies, waits for them, and re-layouts  2.46 us (4%)
    pallas_call x1, Pallas kernels, per_device(): pl.pallas_call(functools.partial(kernel, n_blk, n_tp), out_shape=jax.Shap...  67.4 us
    unnamed x1, local copies, waits for them, and re-layouts  2.46 us

profile of v3, /device:TPU:0, one launch (start us, length us, event | category | flops | bytes accessed | tf_op | source)
XLA Modules:
  0.0 69.9 jit_solution(16974327047016193631)
XLA Ops:
  0.0 67.4 %shard_map.64 = bf16[256,2560]{1,0:T(8,128)(2,1)} custom-call(bf16[256,2560]{1,0:T(8,128)(2,1)} %x_hbm.1, f32[1,5120]{1,0:T(1,128)} %bitcast.1, bf16[5120,384]{1,0:T(8,128)(2,1)} %wq_hbm.1, bf16[384,5120]{1,0:T(8,128)(2,1)} %wo_hbm.1, bf16[384,384]{1,0:T(8,128)(2,1)} %k_hbm.1, bf16[384,384]{1,0:T(8,128)(2,1)} %v_hbm.1), custom_call_target="tpu_custom_call" | custom-call | tf_op jit(solution)/shard_map/pallas_call | solution.py:519
  67.4 2.5 %copy.8 = bf16[256,2560]{1,0:T(8,128)(2,1)} copy(bf16[256,2560]{1,0:T(8,128)(2,1)} %shard_map.64) | data formatting | bytes 2621440
